TPU v7x, 32 devices: a whole 2x2x4 slice. The times are simulated.
32 devices in a mesh: outer: 4 (over z), inner: 8 (over y, x, core).
Axes of the slice: x: 2, y: 2, z: 4, core: 2. Of those that a mesh axis runs over, the one named last changes fastest.
Arguments:
- query_proj: bfloat16 [2048, 8192], P(('outer', 'inner')), may hold values from -8 to 8
- key_proj: bfloat16 [2048, 512], P(('outer', 'inner')), may hold values from -8 to 8
- value_proj: bfloat16 [2048, 512], P(('outer', 'inner')), may hold values from -6 to 6
- positions: int32 [2048], P(('outer', 'inner')), may hold values from 0 to 2047, each once
Outputs:
- attended: bfloat16 [2048, 8192], P(('outer', 'inner'))
Inputs may be any that keep to these rules, and one draw needn't show every extreme that they name: `positions`: each position from 0 to 2047 appears exactly once.
All inputs are finite; a program needn't handle non-finite values.
Results may differ from a plain program's by a relative error of at most 0.005.
Values may be sent and summed in bfloat16 or wider, within the bound.
A program may use at most 64 MiB of HBM per device.

v0:
```python
import math

import jax
import jax.numpy as jnp
from jax import lax
from jax.sharding import PartitionSpec as P

HEAD_WIDTH = 128


masked_score = -1e30


def update(carried, key_value_block, key_pos, query_cluster, query_pos):
    running_top, running_sum, accumulated = carried
    heads_kv = query_cluster.shape[0]
    head_dim = query_cluster.shape[2]
    width = heads_kv * head_dim
    rows_kv = key_value_block.shape[0]
    key_slice = key_value_block[:, :width].reshape(rows_kv, heads_kv, head_dim)
    value_slice = key_value_block[:, width:].reshape(rows_kv, heads_kv, head_dim)
    scores = jnp.einsum(
        "lva,vga->vlg", key_slice, query_cluster, preferred_element_type=jnp.float32
    ) * (1.0 / math.sqrt(head_dim))
    visible = key_pos[None, :, None] <= query_pos[None, None, :]
    block_top = jnp.max(jnp.where(visible, scores, masked_score), axis=1)
    new_top = jnp.maximum(running_top, block_top)
    softmax_weights = jnp.where(visible, jnp.exp(scores - new_top[:, None, :]), 0.0)
    rescale = jnp.exp(running_top - new_top)
    running_sum = running_sum * rescale + jnp.sum(softmax_weights, axis=1)
    accumulated = accumulated * rescale[:, :, None] + jnp.einsum(
        "goi,ogt->git",
        softmax_weights.astype(jnp.bfloat16),
        value_slice,
        preferred_element_type=jnp.float32,
    )
    return (new_top, running_sum, accumulated)


def make_folder(query_cluster, query_pos):

    def fold_piece(carried, kv_piece, first_row):
        kv_rows, key_pos = kv_piece
        row_count = kv_rows.shape[0]
        sub_rows = math.gcd(row_count, 512)
        stacked = kv_rows.reshape(row_count // sub_rows, sub_rows, kv_rows.shape[1])
        pos_stack = key_pos.reshape(row_count // sub_rows, sub_rows)

        def inner_step(carry_in, sub_block):
            return (update(carry_in, sub_block[0], sub_block[1], query_cluster, query_pos), None)

        carried, unused = lax.scan(inner_step, carried, (stacked, pos_stack))
        return carried

    return fold_piece


def start_state(heads_kv, query_rows, head_dim):
    return (
        jnp.full((heads_kv, query_rows), masked_score, jnp.float32),
        jnp.zeros((heads_kv, query_rows), jnp.float32),
        jnp.zeros((heads_kv, query_rows, head_dim), jnp.float32),
    )


def finish(carried):
    return carried[2] / carried[1][:, :, None]


def body(query_proj, key_proj, value_proj, positions):
    tok_rows = query_proj.shape[0]
    head_dim = HEAD_WIDTH
    heads_all = query_proj.shape[1] // head_dim
    heads_kv = key_proj.shape[1] // head_dim
    group_size = heads_all // heads_kv
    inner_count = lax.axis_size("inner")
    per_device = heads_all // inner_count
    repeat_count = group_size // per_device
    key_spread = jnp.repeat(key_proj.reshape(tok_rows, heads_kv, head_dim), repeat_count, axis=1)
    value_broadcast = jnp.repeat(
        value_proj.reshape(tok_rows, heads_kv, head_dim), repeat_count, axis=1
    )
    kv_spread = jnp.concatenate([key_spread, value_broadcast], axis=2).reshape(
        tok_rows, inner_count * 2 * head_dim
    )
    query_heads, kv_heads = (
        lax.all_to_all(query_proj, "inner", split_axis=1, concat_axis=0, tiled=True),
        lax.all_to_all(kv_spread, "inner", split_axis=1, concat_axis=0, tiled=True),
    )
    group_pos = lax.all_gather(positions, "inner", axis=0, tiled=True)
    group_rows = query_heads.shape[0]
    query_cluster = (
        query_heads.reshape(group_rows, per_device, head_dim)
        .transpose(1, 0, 2)
        .reshape(1, per_device * group_rows, head_dim)
    )
    query_pos = jnp.tile(group_pos, per_device)
    folder = make_folder(query_cluster, query_pos)
    initial = start_state(1, per_device * group_rows, head_dim)
    carried = folder(
        initial,
        (
            lax.all_gather(kv_heads, "outer", axis=0, tiled=True),
            lax.all_gather(group_pos, "outer", axis=0, tiled=True),
        ),
        jnp.int32(0),
    )
    result = (
        finish(carried)
        .reshape(per_device, group_rows, head_dim)
        .transpose(1, 0, 2)
        .reshape(group_rows, per_device * head_dim)
        .astype(jnp.bfloat16)
    )
    return lax.all_to_all(result, "inner", split_axis=0, concat_axis=1, tiled=True)


def solution(mesh):
    return jax.shard_map(
        body,
        mesh=mesh,
        in_specs=(
            P(("outer", "inner"), None),
            P(("outer", "inner"), None),
            P(("outer", "inner"), None),
            P(("outer", "inner")),
        ),
        out_specs=P(("outer", "inner"), None),
        check_vma=False,
    )
```

profile of v0, /device:TPU:0, one launch (start us, length us, event | category | flops | bytes accessed | tf_op | source)
XLA Modules:
  0.0 115.0 jit_solution(7399036608634765369)
XLA Ops:
  6.5 0.8 copy-done
  7.4 0.9 copy_bitcast_fusion.2
  8.3 12.0 %all_to_all.48 = bf16[64,8,256]{2,0,1:T(8,128)(2,1)} all-to-all(bf16[64,8,256]{2,0,1:T(8,128)(2,1)S(1)} %pad_maximum_fusion), channel_id=1, replica_groups=mesh['outer'=4,'inner'=8] {'inner'}, dimensions={1} | all-to-all | bytes 524288 | tf_op jit(solution)/shard_map/all_to_all | solution.py:88
  20.4 2.3 %copy.35 = bf16[8,8,8,1024]{3,2,0,1:T(8,128)(2,1)} copy(bf16[8,8,8,1024]{3,2,1,0:T(8,128)(2,1)} %bitcast.91) | data formatting | bytes 2097152 | tf_op jit(solution)/shard_map/all_to_all | solution.py:87
  22.7 3.6 %all-to-all-start.1 = ((bf16[64,8,1024]{2,0,1:T(8,128)(2,1)}), bf16[64,8,1024]{2,0,1:T(8,128)(2,1)S(1)}, u32[]{:S(2)}, u32[]{:S(2)}) async-start(bf16[64,8,1024]{2,0,1:T(8,128)(2,1)} %bitcast.56), calls=%async_computation.1 | async-start | bytes 2097152 | tf_op jit(solution)/shard_map/all_to_all | solution.py:87
  26.3 1.3 %dynamic-slice = u32[1]{0:T(128)} dynamic-slice(u32[32]{0:T(128)} %constant.26, u32[]{:T(128)S(6)} %add.9), dynamic_slice_sizes={1} | dynamic-slice | bytes 12
  28.3 0.9 dynamic-update-slice
  29.1 14.7 %all-reduce = s32[512]{0:T(512)S(1)} all-reduce(s32[512]{0:T(512)S(1)} %dynamic-update-slice), channel_id=1, replica_groups=mesh['outer'=4,'inner'=8] {'inner'}, use_global_device_ids=true, to_apply=%add | all-reduce | flops 512 | bytes 4096
  43.8 12.1 %all-gather = s32[4,1,512]{2,1,0:T(1,128)S(1)} all-gather(s32[1,1,512]{2,1,0:T(1,128)S(1)} %bitcast.102), channel_id=1, replica_groups=mesh['outer'=4,'inner'=8] {'outer'}, dimensions={0}, use_global_device_ids=true | all-gather | bytes 10240 | tf_op jit(solution)/shard_map/all_gather | solution.py:104
  55.9 0.3 copy.29
  56.4 31.0 %while.15 = (s32[]{:T(128)}, f32[1,4096]{1,0:T(1,128)S(1)}, f32[1,4096]{1,0:T(1,128)S(1)}, f32[1,4096,128]{2,1,0:T(8,128)S(1)}, s32[4,512]{1,0:T(4,128)S(1)}, /*...) while((s32[]{:T(128)}, f32[1,4096]{1,0:T(1,128)S(1)}, ...), condition=%wide.region_3.4_spmd.clone, body=%wide.region_0.3_spmd.clone.sunk | while | flops 1104695296 | bytes 31568000 | solution.py:52
  56.5 1.0 dynamic-slice_bitcast_fusion.2
  57.4 1.4 %fusion.31 = (f32[4096]{0:T(1024)S(1)}, f32[512,4096]{1,0:T(8,128)S(1)}) fusion(s32[4096]{0:T(1024)S(1)} %bitcast.86, s32[512]{0:T(512)S(1)} %bitcast.99, bf16[1,4096,128]{2,1,0:T(8,128)(2,1)S(1)} %get-tuple-element.183, bf16[512,256]{1,0:T(8,128)(2,1)S(1)} %dynamic-slice_bitcast_fusion.2), kind=kOutput, calls=%fused_computation.3.clone.1 | convolution fusion | flops 545255424 | bytes 9603072 | tf_op jit(solution)/shard_map/while/body/eval_jaxpr/lva,vga->vlg/dot_general | solution.py:22
  58.9 2.2 %fusion.33 = f32[4096]{0:T(1024)S(1)} fusion(f32[512,4096]{1,0:T(8,128)S(1)} %get-tuple-element.154, f32[4096]{0:T(1024)S(1)} %bitcast.79, s32[4096]{0:T(1024)S(1)} %bitcast.87, s32[512]{0:T(512)S(1)} %bitcast.100), kind=kLoop, calls=%fused_computation.5.clone.1 | loop fusion | flops 10481664 | bytes 8439808 | tf_op jit(solution)/shard_map/while/body/eval_jaxpr/reduce_sum | solution.py:30
  61.2 3.0 %fusion.35 = f32[1,4096,128]{2,1,0:T(8,128)S(1)} fusion(f32[512,4096]{1,0:T(8,128)S(1)} %get-tuple-element.154, f32[4096]{0:T(1024)S(1)} %bitcast.80, s32[4096]{0:T(1024)S(1)} %bitcast.88, s32[512]{0:T(512)S(1)} %bitcast.101, f32[1,4096,128]{2,1,0:T(8,128)S(1)} %get-tuple-element.170, f32[4096]{0:T(1024)S(1)} %bitcast.98, pred[]{:T(512)S(6)} %compare.3, ...), kind=kOutput, calls=%fused_computation.7.clone.1 | convolution fusion | flops 548929536 | bytes 12765185 | tf_op jit(solution)/shard_map/while/body/eval_jaxpr/goi,ogt->git/dot_general | solution.py:31
  64.2 1.0 dynamic-slice_bitcast_fusion.2
  65.2 1.4 %fusion.31 = (f32[4096]{0:T(1024)S(1)}, f32[512,4096]{1,0:T(8,128)S(1)}) fusion(s32[4096]{0:T(1024)S(1)} %bitcast.86, s32[512]{0:T(512)S(1)} %bitcast.99, bf16[1,4096,128]{2,1,0:T(8,128)(2,1)S(1)} %get-tuple-element.183, bf16[512,256]{1,0:T(8,128)(2,1)S(1)} %dynamic-slice_bitcast_fusion.2), kind=kOutput, calls=%fused_computation.3.clone.1 | convolution fusion | flops 545255424 | bytes 9603072 | tf_op jit(solution)/shard_map/while/body/eval_jaxpr/lva,vga->vlg/dot_general | solution.py:22
  66.6 2.2 %fusion.33 = f32[4096]{0:T(1024)S(1)} fusion(f32[512,4096]{1,0:T(8,128)S(1)} %get-tuple-element.154, f32[4096]{0:T(1024)S(1)} %bitcast.79, s32[4096]{0:T(1024)S(1)} %bitcast.87, s32[512]{0:T(512)S(1)} %bitcast.100), kind=kLoop, calls=%fused_computation.5.clone.1 | loop fusion | flops 10481664 | bytes 8439808 | tf_op jit(solution)/shard_map/while/body/eval_jaxpr/reduce_sum | solution.py:30
  68.9 3.0 %fusion.35 = f32[1,4096,128]{2,1,0:T(8,128)S(1)} fusion(f32[512,4096]{1,0:T(8,128)S(1)} %get-tuple-element.154, f32[4096]{0:T(1024)S(1)} %bitcast.80, s32[4096]{0:T(1024)S(1)} %bitcast.88, s32[512]{0:T(512)S(1)} %bitcast.101, f32[1,4096,128]{2,1,0:T(8,128)S(1)} %get-tuple-element.170, f32[4096]{0:T(1024)S(1)} %bitcast.98, pred[]{:T(512)S(6)} %compare.3, ...), kind=kOutput, calls=%fused_computation.7.clone.1 | convolution fusion | flops 548929536 | bytes 12765185 | tf_op jit(solution)/shard_map/while/body/eval_jaxpr/goi,ogt->git/dot_general | solution.py:31
  71.9 1.0 dynamic-slice_bitcast_fusion.2
  72.9 1.4 %fusion.31 = (f32[4096]{0:T(1024)S(1)}, f32[512,4096]{1,0:T(8,128)S(1)}) fusion(s32[4096]{0:T(1024)S(1)} %bitcast.86, s32[512]{0:T(512)S(1)} %bitcast.99, bf16[1,4096,128]{2,1,0:T(8,128)(2,1)S(1)} %get-tuple-element.183, bf16[512,256]{1,0:T(8,128)(2,1)S(1)} %dynamic-slice_bitcast_fusion.2), kind=kOutput, calls=%fused_computation.3.clone.1 | convolution fusion | flops 545255424 | bytes 9603072 | tf_op jit(solution)/shard_map/while/body/eval_jaxpr/lva,vga->vlg/dot_general | solution.py:22
  74.4 2.2 %fusion.33 = f32[4096]{0:T(1024)S(1)} fusion(f32[512,4096]{1,0:T(8,128)S(1)} %get-tuple-element.154, f32[4096]{0:T(1024)S(1)} %bitcast.79, s32[4096]{0:T(1024)S(1)} %bitcast.87, s32[512]{0:T(512)S(1)} %bitcast.100), kind=kLoop, calls=%fused_computation.5.clone.1 | loop fusion | flops 10481664 | bytes 8439808 | tf_op jit(solution)/shard_map/while/body/eval_jaxpr/reduce_sum | solution.py:30
  76.7 3.0 %fusion.35 = f32[1,4096,128]{2,1,0:T(8,128)S(1)} fusion(f32[512,4096]{1,0:T(8,128)S(1)} %get-tuple-element.154, f32[4096]{0:T(1024)S(1)} %bitcast.80, s32[4096]{0:T(1024)S(1)} %bitcast.88, s32[512]{0:T(512)S(1)} %bitcast.101, f32[1,4096,128]{2,1,0:T(8,128)S(1)} %get-tuple-element.170, f32[4096]{0:T(1024)S(1)} %bitcast.98, pred[]{:T(512)S(6)} %compare.3, ...), kind=kOutput, calls=%fused_computation.7.clone.1 | convolution fusion | flops 548929536 | bytes 12765185 | tf_op jit(solution)/shard_map/while/body/eval_jaxpr/goi,ogt->git/dot_general | solution.py:31
  79.7 1.0 dynamic-slice_bitcast_fusion.2
  80.7 1.4 %fusion.31 = (f32[4096]{0:T(1024)S(1)}, f32[512,4096]{1,0:T(8,128)S(1)}) fusion(s32[4096]{0:T(1024)S(1)} %bitcast.86, s32[512]{0:T(512)S(1)} %bitcast.99, bf16[1,4096,128]{2,1,0:T(8,128)(2,1)S(1)} %get-tuple-element.183, bf16[512,256]{1,0:T(8,128)(2,1)S(1)} %dynamic-slice_bitcast_fusion.2), kind=kOutput, calls=%fused_computation.3.clone.1 | convolution fusion | flops 545255424 | bytes 9603072 | tf_op jit(solution)/shard_map/while/body/eval_jaxpr/lva,vga->vlg/dot_general | solution.py:22
  82.1 2.2 %fusion.33 = f32[4096]{0:T(1024)S(1)} fusion(f32[512,4096]{1,0:T(8,128)S(1)} %get-tuple-element.154, f32[4096]{0:T(1024)S(1)} %bitcast.79, s32[4096]{0:T(1024)S(1)} %bitcast.87, s32[512]{0:T(512)S(1)} %bitcast.100), kind=kLoop, calls=%fused_computation.5.clone.1 | loop fusion | flops 10481664 | bytes 8439808 | tf_op jit(solution)/shard_map/while/body/eval_jaxpr/reduce_sum | solution.py:30
  84.4 3.0 %fusion.35 = f32[1,4096,128]{2,1,0:T(8,128)S(1)} fusion(f32[512,4096]{1,0:T(8,128)S(1)} %get-tuple-element.154, f32[4096]{0:T(1024)S(1)} %bitcast.80, s32[4096]{0:T(1024)S(1)} %bitcast.88, s32[512]{0:T(512)S(1)} %bitcast.101, f32[1,4096,128]{2,1,0:T(8,128)S(1)} %get-tuple-element.170, f32[4096]{0:T(1024)S(1)} %bitcast.98, pred[]{:T(512)S(6)} %compare.3, ...), kind=kOutput, calls=%fused_computation.7.clone.1 | convolution fusion | flops 548929536 | bytes 12765185 | tf_op jit(solution)/shard_map/while/body/eval_jaxpr/goi,ogt->git/dot_general | solution.py:31
  87.4 0.7 divide_convert_fusion
  88.1 0.7 copy.36
  88.8 0.5 convert_element_type.20
  89.3 17.8 %all_to_all.49 = bf16[8,64,1024]{2,1,0:T(8,128)(2,1)S(1)} all-to-all(bf16[8,64,1024]{2,1,0:T(8,128)(2,1)S(1)} %convert_element_type.20), channel_id=1, replica_groups=mesh['outer'=4,'inner'=8] {'inner'}, dimensions={0} | all-to-all | bytes 2097152 | tf_op jit(solution)/shard_map/all_to_all | solution.py:115
  107.1 1.1 copy.28
  (39 shorter events, 0.7 us)
Async XLA Ops:
  6.5 0.8 copy-start
  6.5 49.9 %all-gather.3.cloned.1.call-start = ((), (), s32[]{:S(2)}) async-start(), calls=%async_computation.3 | async-start | bytes 1310720 | tf_op jit(solution)/shard_map/all_gather | solution.py:103
  22.7 33.3 %all-to-all-start.1 = ((bf16[64,8,1024]{2,0,1:T(8,128)(2,1)}), bf16[64,8,1024]{2,0,1:T(8,128)(2,1)S(1)}, u32[]{:S(2)}, u32[]{:S(2)}) async-start(bf16[64,8,1024]{2,0,1:T(8,128)(2,1)} %bitcast.56), calls=%async_computation.1 | async-start | bytes 2097152 | tf_op jit(solution)/shard_map/all_to_all | solution.py:87
Sparse Core Ops, SparseCore 0:
  20.5 27.3 all-gather.2
where the time goes:
time: 116 us; the launch traced here: 115 us
  blocking collectives  56.6 us (49%)
  matrix products  17.6 us (15%)
  between operations  14.2 us (12%)
  local copies, waits for them, and re-layouts  12.8 us (11%)
  other arithmetic  9.87 us (9%)
  starting transfers between devices  3.56 us (3%)
    all_to_all x1, blocking collectives, body(): lax.all_to_all(result, 'inner', split_axis=0, concat_axis=1, tiled=True)  17.8 us
    unnamed x1, blocking collectives  14.7 us
    all_gather x1, blocking collectives, body(): lax.all_gather(group_pos, 'outer', axis=0, tiled=True)  12.1 us
    all_to_all x1, blocking collectives, body(): lax.all_to_all(kv_spread, 'inner', split_axis=1, concat_axis=0, tiled=True)  12 us
    dot_general x4, matrix products, update(): jnp.einsum('goi,ogt->git', softmax_weights.astype(jnp.bfloat16), value_sl...  11.9 us
    reduce_sum x4, other arithmetic, update(): running_sum = running_sum * rescale + jnp.sum(softmax_weights, axis=1)  8.73 us
    dot_general x4, matrix products, update(): jnp.einsum('lva,vga->vlg', key_slice, query_cluster, preferred_element_ty...  5.72 us
    squeeze x4, local copies, waits for them, and re-layouts, fold_piece(): carried, unused = lax.scan(inner_step, carried, (stacked, pos_stack))  3.9 us
  transfers between devices with their start and end apart: 2, of which 0 were waited for; matrix products, arithmetic and copies ran while one was open for 4% of the time, Pallas kernels for 0%

commit v1 on v0

v1 whole, which is shorter than its diff:
```python
import functools
import math

import jax
import jax.numpy as jnp
from jax import lax
from jax.experimental import pallas as pl
from jax.experimental.pallas import tpu as pltpu
from jax.sharding import PartitionSpec as P

HEAD_WIDTH = 128
HIDDEN = -1e30


def kernel(sizes, q_ref, k_ref, v_ref, pos_ref, out_ref, buf, pbuf, mask, top, acc,
           copy_sem, recv_sem, send_sem):
    nz, ny, nx, rows, heads_kv, group = sizes
    d = HEAD_WIDTH
    half_heads = heads_kv // 2
    wide = half_heads * d
    chips = ny * nx
    slots = 2 * chips
    keys = slots * rows
    z = lax.axis_index("outer")
    inner = lax.axis_index("inner")
    core = lax.rem(inner, 2)
    x = lax.rem(inner // 2, nx)
    y = inner // (2 * nx)

    def dev(dz=0, dy=0, dx=0, dc=0):
        zz = lax.rem(z + dz, nz)
        yy = lax.rem(y + dy, ny)
        xx = lax.rem(x + dx, nx)
        cc = lax.rem(core + dc, 2)
        return (zz, (yy * nx + xx) * 2 + cc)

    def slot(dx, dy, dc):
        return (dc * ny + dy) * nx + dx

    local = []
    for half in range(2):
        cols = pl.ds(half * wide, wide)
        for part, ref in enumerate((k_ref, v_ref)):
            local.append(pltpu.make_async_copy(
                ref.at[:, cols], buf.at[0, half, 0, :, pl.ds(part * wide, wide)],
                copy_sem.at[2 * half + part]))
    local.append(pltpu.make_async_copy(pos_ref, pbuf.at[0, 0], copy_sem.at[4]))
    for c in local:
        c.start()

    barrier = pltpu.get_barrier_semaphore()
    peers = [dict(dz=i) for i in range(1, nz)] + [dict(dy=i) for i in range(1, ny)]
    peers += [dict(dx=i) for i in range(1, nx)] + [dict(dc=1)]
    for peer in peers:
        pl.semaphore_signal(barrier, inc=1, device_id=dev(**peer),
                            device_id_type=pl.DeviceIdType.MESH)
    pl.semaphore_wait(barrier, len(peers))
    for c in local:
        c.wait()

    sent = []

    def ref_of(s, kind, sl):
        return pbuf.at[s, sl] if kind == 2 else buf.at[s, kind, sl]

    def send(src, dst, to):
        n = len(sent)
        c = pltpu.make_async_remote_copy(
            src_ref=ref_of(*src), dst_ref=ref_of(*dst), send_sem=send_sem.at[n],
            recv_sem=recv_sem.at[dst[0], dst[1], dst[2]], device_id=dev(**to),
            device_id_type=pl.DeviceIdType.MESH)
        c.start()
        sent.append(c)

    def arrived(s, kind, sl):
        r = ref_of(s, kind, sl)
        pltpu.make_async_remote_copy(
            src_ref=r, dst_ref=r, send_sem=send_sem.at[0],
            recv_sem=recv_sem.at[s, kind, sl], device_id=dev(dc=1),
            device_id_type=pl.DeviceIdType.MESH).wait_recv()

    KINDS = (2, 0, 1)

    def issue_column(s):
        for kind in KINDS:
            if s:
                arrived(s, kind, 0)
            src = (s, kind, 0)
            order = ("x", "y") if kind != 1 else ("y", "x")
            for axis in order:
                if axis == "x":
                    for dx in range(1, nx):
                        send(src, (s, kind, slot(dx, 0, 0)), dict(dx=dx))
                else:
                    for dy in range(1, ny):
                        send(src, (s, kind, slot(0, dy, 0)), dict(dy=dy))
            send(src, (s, kind, slot(0, 0, 1)), dict(dc=1))

    def to_sibling(s, kind, dx, dy):
        send((s, kind, slot(dx, dy, 0)), (s, kind, slot(dx, dy, 1)), dict(dc=1))

    def relay(s):
        for kind in (2, 0):
            for dx in range(1, nx):
                here = slot(dx, 0, 0)
                arrived(s, kind, here)
                for dy in range(1, ny):
                    send((s, kind, here), (s, kind, slot(dx, dy, 0)), dict(dy=dy))
                to_sibling(s, kind, dx, 0)
        for dy in range(1, ny):
            here = slot(0, dy, 0)
            arrived(s, 1, here)
            for dx in range(1, nx):
                send((s, 1, here), (s, 1, slot(dx, dy, 0)), dict(dx=dx))
            to_sibling(s, 1, 0, dy)
        for dx in range(1, nx):
            arrived(s, 1, slot(dx, 0, 0))
            to_sibling(s, 1, dx, 0)
        for kind in (2, 0):
            for dy in range(1, ny):
                arrived(s, kind, slot(0, dy, 0))
                to_sibling(s, kind, 0, dy)

    def gather_rest(s):
        for kind in KINDS:
            for dy in range(1, ny):
                for dx in range(1, nx):
                    arrived(s, kind, slot(dx, dy, 0))
                    to_sibling(s, kind, dx, dy)
        for kind in KINDS:
            for sl in range(chips, slots):
                arrived(s, kind, sl)

    def build_mask(s):
        mine = jnp.concatenate([pos_ref[...], pos_ref[...]], axis=1)
        mine = jnp.broadcast_to(mine.astype(jnp.float32), (rows, 2 * rows))
        for sl in range(slots):
            theirs = jnp.broadcast_to(pbuf[s, sl].astype(jnp.float32), (2 * rows, rows)).T
            mask[sl * rows:(sl + 1) * rows, :] = jnp.where(
                theirs > mine, HIDDEN, 0.0).astype(jnp.bfloat16)

    eye = (lax.broadcasted_iota(jnp.int32, (rows, 2 * rows), 0)
           == lax.broadcasted_iota(jnp.int32, (rows, 2 * rows), 1)).astype(jnp.bfloat16)
    scale = math.log2(math.e) / math.sqrt(d)
    per_tile = math.gcd(4, group)
    tile = per_tile * rows
    tiles = group // per_tile

    def one_tile(s, half, hh, t):
        head = half * half_heads + hh
        first = head * group + t * per_tile
        at = pl.multiple_of(first * rows, tile)
        query = jnp.concatenate(
            [jnp.concatenate(
                [q_ref[:, pl.ds(pl.multiple_of((first + j) * d, d), d)], eye], axis=1)
             for j in range(per_tile)], axis=0)
        k_tile = buf[s, half, :, :, hh * d:(hh + 1) * d].reshape(keys, d)
        v_tile = buf[s, half, :, :, wide + hh * d:wide + (hh + 1) * d].reshape(keys, d)
        k_wide = jnp.concatenate([k_tile, mask[...]], axis=1)
        v_wide = jnp.concatenate([v_tile, jnp.ones((keys, d), jnp.bfloat16)], axis=1)
        scores = lax.dot_general(query, k_wide, (((1,), (1,)), ((), ())),
                                 preferred_element_type=jnp.float32)
        block_top = jnp.max(scores, axis=1, keepdims=True)
        window = pl.ds(at, tile)
        if s == 0:
            new_top = block_top
        else:
            old_top = top[window, :1]
            new_top = jnp.maximum(old_top, block_top)
            rescale = jnp.exp2((old_top - new_top) * scale)
        weights = jnp.exp2((scores - new_top) * scale).astype(jnp.bfloat16)
        got = lax.dot_general(weights, v_wide, (((1,), (0,)), ((), ())),
                              preferred_element_type=jnp.float32)
        if s:
            got = acc[window, :] * rescale + got
        if s < nz - 1:
            acc[window, :] = got
            top[window, :] = jnp.broadcast_to(new_top, (tile, d))
        else:
            result = (got[:, :d] / got[:, d:]).astype(jnp.bfloat16)
            for j in range(per_tile):
                out_ref[:, pl.ds(pl.multiple_of((first + j) * d, d), d)] = (
                    result[j * rows:(j + 1) * rows, :])

    def compute(s, half):
        for hh in range(half_heads):
            @pl.loop(0, tiles // 2)
            def _(t):
                for u in range(2):
                    one_tile(s, half, hh, t * 2 + u)

    for dz in range(1, nz):
        for kind in KINDS:
            send((0, kind, 0), (dz, kind, 0), dict(dz=dz))
            if dz == 1:
                pass
    issue_column(0)
    relay(0)
    issue_column(1)
    for s in range(nz):
        gather_rest(s)
        build_mask(s)
        compute(s, 0)
        if s + 1 < nz:
            relay(s + 1)
        if s + 2 < nz:
            issue_column(s + 2)
        compute(s, 1)
    for c in sent:
        c.wait_send()


def body(query_proj, key_proj, value_proj, positions):
    rows, width = query_proj.shape
    d = HEAD_WIDTH
    heads_kv = key_proj.shape[1] // d
    group = width // d // heads_kv
    nz = lax.axis_size("outer")
    inner = lax.axis_size("inner")
    nx = 2
    ny = inner // 4
    slots = inner
    sizes = (nz, ny, nx, rows, heads_kv, group)
    wide = heads_kv // 2 * d
    copies = 3 * (nz - 1) + nz * (3 * (nx - 1 + ny - 1 + slots // 2) + 3 * (nx - 1) * (ny - 1))
    return pl.pallas_call(
        functools.partial(kernel, sizes),
        out_shape=jax.ShapeDtypeStruct((rows, width), jnp.bfloat16),
        in_specs=[pl.BlockSpec(memory_space=pltpu.VMEM), pl.BlockSpec(memory_space=pl.ANY),
                  pl.BlockSpec(memory_space=pl.ANY), pl.BlockSpec(memory_space=pltpu.VMEM)],
        out_specs=pl.BlockSpec(memory_space=pltpu.VMEM),
        scratch_shapes=[
            pltpu.VMEM((nz, 2, slots, rows, 2 * wide), jnp.bfloat16),
            pltpu.VMEM((nz, slots, 1, rows), jnp.int32),
            pltpu.VMEM((slots * rows, d), jnp.bfloat16),
            pltpu.VMEM((width // d * rows, d), jnp.float32),
            pltpu.VMEM((width // d * rows, 2 * d), jnp.float32),
            pltpu.SemaphoreType.DMA((5,)),
            pltpu.SemaphoreType.DMA((nz, 3, slots)),
            pltpu.SemaphoreType.DMA((copies,)),
        ],
        compiler_params=pltpu.CompilerParams(
            collective_id=0, has_side_effects=True, vmem_limit_bytes=56 * 1024 * 1024),
    )(query_proj, key_proj, value_proj, positions.reshape(1, rows))


def solution(mesh):
    return jax.shard_map(
        body,
        mesh=mesh,
        in_specs=(
            P(("outer", "inner"), None),
            P(("outer", "inner"), None),
            P(("outer", "inner"), None),
            P(("outer", "inner")),
        ),
        out_specs=P(("outer", "inner"), None),
        check_vma=False,
    )
```

time: 116 us -> 55.4 us (0.48)
  blocking collectives: 56.6 us -> 0 us
  Pallas kernels: 0 us -> 52.9 us
  matrix products: 17.6 us -> 0 us
  between operations: 14.2 us -> 0.01 us
  local copies, waits for them, and re-layouts: 12.8 us -> 2.26 us
  other arithmetic: 9.87 us -> 0 us
  starting transfers between devices: 3.56 us -> 0 us
    pallas_call x0 -> x1, Pallas kernels: none -> 52.9 us  [body(): pl.pallas_call(functools.partial(kernel, sizes), out_shape=jax.ShapeDtype...]
    all_to_all x2 -> x0, blocking collectives: 29.8 us -> none  [the longest x1 17.8 us: body(): lax.all_to_all(result, 'inner', split_axis=0, concat_axis=1, tiled=True)]
    dot_general x8 -> x0, matrix products: 17.6 us -> none  [the longest x4 11.9 us: update(): jnp.einsum('goi,ogt->git', softmax_weights.astype(jnp.bfloat16), value_sl...]
    unnamed x1 -> x0, blocking collectives: 14.7 us -> none
    all_gather x1 -> x0, blocking collectives: 12.1 us -> none  [body(): lax.all_gather(group_pos, 'outer', axis=0, tiled=True)]
    reduce_sum x4 -> x0, other arithmetic: 8.73 us -> none  [update(): running_sum = running_sum * rescale + jnp.sum(softmax_weights, axis=1)]
    squeeze x4 -> x0, local copies, waits for them, and re-layouts: 3.9 us -> none  [fold_piece(): carried, unused = lax.scan(inner_step, carried, (stacked, pos_stack))]
    all_to_all x1 -> x0, starting transfers between devices: 3.56 us -> none  [body(): lax.all_to_all(query_proj, 'inner', split_axis=1, concat_axis=0, tiled=True)]
  transfers between devices with their start and end apart: 2 -> 0, of which waited for: 0 -> 0; matrix products, arithmetic and copies ran while one was open for 4% -> 0% of each run, Pallas kernels for 0% -> 0%
where the time goes in v1:
time: 55.4 us; the launch traced here: 55.2 us
  Pallas kernels  52.9 us (95%)
  local copies, waits for them, and re-layouts  2.26 us (4%)
    pallas_call x1, Pallas kernels, body(): pl.pallas_call(functools.partial(kernel, sizes), out_shape=jax.ShapeDtype...  52.9 us
    unnamed x1, local copies, waits for them, and re-layouts  2.26 us

profile of v1, /device:TPU:0, one launch (start us, length us, event | category | flops | bytes accessed | tf_op | source)
XLA Modules:
  0.0 55.2 jit_solution(15331920388159927051)
XLA Ops:
  0.0 52.9 %shard_map.46 = bf16[64,8192]{1,0:T(8,128)(2,1)} custom-call(bf16[64,8192]{1,0:T(8,128)(2,1)} %q_ref.1, bf16[64,512]{1,0:T(8,128)(2,1)} %k_ref.1, bf16[64,512]{1,0:T(8,128)(2,1)} %v_ref.1, s32[1,64]{1,0:T(1,128)} %bitcast.1), custom_call_target="tpu_custom_call" | custom-call | tf_op jit(solution)/shard_map/pallas_call | solution.py:226
  52.9 2.3 %copy.6 = bf16[64,8192]{1,0:T(8,128)(2,1)} copy(bf16[64,8192]{1,0:T(8,128)(2,1)} %shard_map.46) | data formatting | bytes 2097152

commit v2 on v1

--- a/solution.py
+++ b/solution.py
@@ -13,7 +13,7 @@
 
 
 def kernel(sizes, q_ref, k_ref, v_ref, pos_ref, out_ref, buf, pbuf, mask, top, acc,
-           copy_sem, recv_sem, send_sem):
+           q_buf, copy_sem, recv_sem, send_sem):
     nz, ny, nx, rows, heads_kv, group = sizes
     d = HEAD_WIDTH
     half_heads = heads_kv // 2
@@ -37,6 +37,7 @@
     def slot(dx, dy, dc):
         return (dc * ny + dy) * nx + dx
 
+    query_copy = pltpu.make_async_copy(q_ref, q_buf, copy_sem.at[5])
     local = []
     for half in range(2):
         cols = pl.ds(half * wide, wide)
@@ -48,8 +49,9 @@
     for c in local:
         c.start()
 
+    query_copy.start()
     barrier = pltpu.get_barrier_semaphore()
-    peers = [dict(dz=i) for i in range(1, nz)] + [dict(dy=i) for i in range(1, ny)]
+    peers = [dict(dz=i) for i in sorted({1 % nz, nz - 1} - {0})] + [dict(dy=i) for i in range(1, ny)]
     peers += [dict(dx=i) for i in range(1, nx)] + [dict(dc=1)]
     for peer in peers:
         pl.semaphore_signal(barrier, inc=1, device_id=dev(**peer),
@@ -86,6 +88,8 @@
             if s:
                 arrived(s, kind, 0)
             src = (s, kind, 0)
+            if s + 1 < nz:
+                send(src, (s + 1, kind, 0), dict(dz=1))
             order = ("x", "y") if kind != 1 else ("y", "x")
             for axis in order:
                 if axis == "x":
@@ -142,70 +146,78 @@
     eye = (lax.broadcasted_iota(jnp.int32, (rows, 2 * rows), 0)
            == lax.broadcasted_iota(jnp.int32, (rows, 2 * rows), 1)).astype(jnp.bfloat16)
     scale = math.log2(math.e) / math.sqrt(d)
-    per_tile = math.gcd(4, group)
+    per_tile = math.gcd(8, group)
     tile = per_tile * rows
     tiles = group // per_tile
 
-    def one_tile(s, half, hh, t):
-        head = half * half_heads + hh
-        first = head * group + t * per_tile
-        at = pl.multiple_of(first * rows, tile)
-        query = jnp.concatenate(
-            [jnp.concatenate(
-                [q_ref[:, pl.ds(pl.multiple_of((first + j) * d, d), d)], eye], axis=1)
-             for j in range(per_tile)], axis=0)
-        k_tile = buf[s, half, :, :, hh * d:(hh + 1) * d].reshape(keys, d)
-        v_tile = buf[s, half, :, :, wide + hh * d:wide + (hh + 1) * d].reshape(keys, d)
-        k_wide = jnp.concatenate([k_tile, mask[...]], axis=1)
-        v_wide = jnp.concatenate([v_tile, jnp.ones((keys, d), jnp.bfloat16)], axis=1)
-        scores = lax.dot_general(query, k_wide, (((1,), (1,)), ((), ())),
-                                 preferred_element_type=jnp.float32)
-        block_top = jnp.max(scores, axis=1, keepdims=True)
-        window = pl.ds(at, tile)
-        if s == 0:
-            new_top = block_top
-        else:
-            old_top = top[window, :1]
-            new_top = jnp.maximum(old_top, block_top)
-            rescale = jnp.exp2((old_top - new_top) * scale)
-        weights = jnp.exp2((scores - new_top) * scale).astype(jnp.bfloat16)
-        got = lax.dot_general(weights, v_wide, (((1,), (0,)), ((), ())),
-                              preferred_element_type=jnp.float32)
-        if s:
-            got = acc[window, :] * rescale + got
-        if s < nz - 1:
-            acc[window, :] = got
-            top[window, :] = jnp.broadcast_to(new_top, (tile, d))
-        else:
-            result = (got[:, :d] / got[:, d:]).astype(jnp.bfloat16)
-            for j in range(per_tile):
-                out_ref[:, pl.ds(pl.multiple_of((first + j) * d, d), d)] = (
-                    result[j * rows:(j + 1) * rows, :])
+    ones = jnp.ones((keys, d), jnp.bfloat16)
 
     def compute(s, half):
-        for hh in range(half_heads):
-            @pl.loop(0, tiles // 2)
-            def _(t):
-                for u in range(2):
-                    one_tile(s, half, hh, t * 2 + u)
-
-    for dz in range(1, nz):
-        for kind in KINDS:
-            send((0, kind, 0), (dz, kind, 0), dict(dz=dz))
-            if dz == 1:
-                pass
+        @pl.loop(0, half_heads)
+        def _(hh):
+            head = half * half_heads + hh
+            k_cols = pl.ds(pl.multiple_of(hh * d, d), d)
+            v_cols = pl.ds(pl.multiple_of(wide + hh * d, d), d)
+            k_wide = jnp.concatenate([buf[s, half, :, :, k_cols].reshape(keys, d), mask[...]],
+                                     axis=1)
+            v_wide = jnp.concatenate([buf[s, half, :, :, v_cols].reshape(keys, d), ones], axis=1)
+
+            def columns(t, j):
+                return pl.ds(pl.multiple_of((head * group + t * per_tile + j) * d, d), d)
+
+            def score(t):
+                query = jnp.concatenate(
+                    [jnp.concatenate([q_buf[:, columns(t, j)], eye], axis=1)
+                     for j in range(per_tile)], axis=0)
+                return lax.dot_general(query, k_wide, (((1,), (1,)), ((), ())),
+                                       preferred_element_type=jnp.float32)
+
+            def fold(t, scores):
+                window = slice(t * tile, (t + 1) * tile)
+                new_top = jnp.broadcast_to(jnp.max(scores, axis=1, keepdims=True), (tile, d))
+                if s:
+                    old_top = top[head, window, :]
+                    new_top = jnp.maximum(old_top, new_top)
+                    rescale = jnp.exp2((old_top - new_top) * scale)
+                weights = jnp.exp2((scores - jnp.concatenate([new_top] * (keys // d), axis=1)) * scale).astype(jnp.bfloat16)
+                got = lax.dot_general(weights, v_wide, (((1,), (0,)), ((), ())),
+                                      preferred_element_type=jnp.float32)
+                if s:
+                    got = acc[head, window, :] * jnp.concatenate([rescale, rescale], axis=1) + got
+                if s < nz - 1:
+                    acc[head, window, :] = got
+                    top[head, window, :] = new_top
+                else:
+                    result = (got[:, :d] / got[:, d:]).astype(jnp.bfloat16)
+                    for j in range(per_tile):
+                        out_ref[:, columns(t, j)] = result[j * rows:(j + 1) * rows, :]
+
+            held = score(0)
+            for t in range(tiles):
+                following = score(t + 1) if t + 1 < tiles else None
+                fold(t, held)
+                held = following
+
     issue_column(0)
     relay(0)
-    issue_column(1)
+    if nz > 1:
+        issue_column(1)
+    gather_rest(0)
+    query_copy.wait()
     for s in range(nz):
-        gather_rest(s)
         build_mask(s)
         compute(s, 0)
+        if s == 0 and nz > 2:
+            issue_column(2)
+        elif 0 < s < nz - 1:
+            relay(s + 1)
+        compute(s, 1)
+        if s == 0 and nz > 1:
+            relay(1)
+        if s + 3 < nz:
+            issue_column(s + 3)
         if s + 1 < nz:
-            relay(s + 1)
-        if s + 2 < nz:
-            issue_column(s + 2)
-        compute(s, 1)
+            gather_rest(s + 1)
     for c in sent:
         c.wait_send()
 
@@ -226,21 +238,22 @@
     return pl.pallas_call(
         functools.partial(kernel, sizes),
         out_shape=jax.ShapeDtypeStruct((rows, width), jnp.bfloat16),
-        in_specs=[pl.BlockSpec(memory_space=pltpu.VMEM), pl.BlockSpec(memory_space=pl.ANY),
+        in_specs=[pl.BlockSpec(memory_space=pl.ANY), pl.BlockSpec(memory_space=pl.ANY),
                   pl.BlockSpec(memory_space=pl.ANY), pl.BlockSpec(memory_space=pltpu.VMEM)],
         out_specs=pl.BlockSpec(memory_space=pltpu.VMEM),
         scratch_shapes=[
             pltpu.VMEM((nz, 2, slots, rows, 2 * wide), jnp.bfloat16),
             pltpu.VMEM((nz, slots, 1, rows), jnp.int32),
             pltpu.VMEM((slots * rows, d), jnp.bfloat16),
-            pltpu.VMEM((width // d * rows, d), jnp.float32),
-            pltpu.VMEM((width // d * rows, 2 * d), jnp.float32),
-            pltpu.SemaphoreType.DMA((5,)),
+            pltpu.VMEM((heads_kv, group * rows, d), jnp.float32),
+            pltpu.VMEM((heads_kv, group * rows, 2 * d), jnp.float32),
+            pltpu.VMEM((rows, width), jnp.bfloat16),
+            pltpu.SemaphoreType.DMA((6,)),
             pltpu.SemaphoreType.DMA((nz, 3, slots)),
             pltpu.SemaphoreType.DMA((copies,)),
         ],
         compiler_params=pltpu.CompilerParams(
-            collective_id=0, has_side_effects=True, vmem_limit_bytes=56 * 1024 * 1024),
+            collective_id=0, has_side_effects=True, vmem_limit_bytes=44 * 1024 * 1024),
     )(query_proj, key_proj, value_proj, positions.reshape(1, rows))
 
 

time: 55.4 us -> 47.1 us (0.85)
  Pallas kernels: 52.9 us -> 42.3 us
  local copies, waits for them, and re-layouts: 2.26 us -> 4.53 us
    pallas_call x1, Pallas kernels: 52.9 us -> 42.3 us  [body(): pl.pallas_call(functools.partial(kernel, sizes), out_shape=jax.ShapeDtype...]
    unnamed x1 -> x9, local copies, waits for them, and re-layouts: 2.26 us -> 4.53 us
where the time goes in v2:
time: 47.1 us; the launch traced here: 46.8 us
  Pallas kernels  42.3 us (90%)
  local copies, waits for them, and re-layouts  4.53 us (10%)
    pallas_call x1, Pallas kernels, body(): pl.pallas_call(functools.partial(kernel, sizes), out_shape=jax.ShapeDtype...  42.3 us
    unnamed x9, local copies, waits for them, and re-layouts  4.53 us

profile of v2, /device:TPU:0, one launch (start us, length us, event | category | flops | bytes accessed | tf_op | source)
XLA Modules:
  0.0 46.8 jit_solution(8447616686470598590)
XLA Ops:
  0.0 0.0 copy-start.3
  0.0 0.7 %copy-done.3 = s32[64]{0:T(128)S(1)} copy-done((s32[64]{0:T(128)S(1)}, s32[64]{0:T(128)}, u32[]{:S(2)}) %copy-start.3) | copy-done | bytes 280
  0.7 0.0 copy-start
  0.7 1.2 %copy-done = bf16[64,8192]{1,0:T(8,128)(2,1)S(1)} copy-done((bf16[64,8192]{1,0:T(8,128)(2,1)S(1)}, bf16[64,8192]{1,0:T(8,128)(2,1)}, u32[]{:S(2)}) %copy-start) | copy-done | bytes 1048600
  1.9 0.0 copy-start.1
  1.9 0.8 %copy-done.1 = bf16[64,512]{1,0:T(8,128)(2,1)S(1)} copy-done((bf16[64,512]{1,0:T(8,128)(2,1)S(1)}, bf16[64,512]{1,0:T(8,128)(2,1)}, u32[]{:S(2)}) %copy-start.1) | copy-done | bytes 65560
  2.7 0.0 copy-start.2
  2.7 0.8 %copy-done.2 = bf16[64,512]{1,0:T(8,128)(2,1)S(1)} copy-done((bf16[64,512]{1,0:T(8,128)(2,1)S(1)}, bf16[64,512]{1,0:T(8,128)(2,1)}, u32[]{:S(2)}) %copy-start.2) | copy-done | bytes 65560
  3.6 42.3 %shard_map.46 = bf16[64,8192]{1,0:T(8,128)(2,1)S(1)} custom-call(bf16[64,8192]{1,0:T(8,128)(2,1)S(1)} %copy-done, bf16[64,512]{1,0:T(8,128)(2,1)S(1)} %copy-done.1, bf16[64,512]{1,0:T(8,128)(2,1)S(1)} %copy-done.2, s32[1,64]{1,0:T(1,128)S(1)} %bitcast.1), custom_call_target="tpu_custom_call" | custom-call | tf_op jit(solution)/shard_map/pallas_call | solution.py:238
  45.8 1.0 %copy.6 = bf16[64,8192]{1,0:T(8,128)(2,1)} copy(bf16[64,8192]{1,0:T(8,128)(2,1)S(1)} %shard_map.46) | data formatting | bytes 2097152
Async XLA Ops:
  0.0 0.7 %copy-start.3 = (s32[64]{0:T(128)S(1)}, s32[64]{0:T(128)}, u32[]{:S(2)}) copy-start(s32[64]{0:T(128)} %param.7) | copy-start | bytes 772
  0.7 1.2 %copy-start = (bf16[64,8192]{1,0:T(8,128)(2,1)S(1)}, bf16[64,8192]{1,0:T(8,128)(2,1)}, u32[]{:S(2)}) copy-start(bf16[64,8192]{1,0:T(8,128)(2,1)} %q_ref.1) | copy-start | bytes 3145732
  1.9 0.8 %copy-start.1 = (bf16[64,512]{1,0:T(8,128)(2,1)S(1)}, bf16[64,512]{1,0:T(8,128)(2,1)}, u32[]{:S(2)}) copy-start(bf16[64,512]{1,0:T(8,128)(2,1)} %k_ref.1) | copy-start | bytes 196612
  2.7 0.8 %copy-start.2 = (bf16[64,512]{1,0:T(8,128)(2,1)S(1)}, bf16[64,512]{1,0:T(8,128)(2,1)}, u32[]{:S(2)}) copy-start(bf16[64,512]{1,0:T(8,128)(2,1)} %v_ref.1) | copy-start | bytes 196612
